TPU v7x, 256 devices: a whole 4x4x8 slice. The times are simulated.
256 devices in a mesh: dp: 32 (over z, x_hi, core), expert: 8 (over x_lo, y).
Axes of the slice: x: 4 (x_hi: 2, x_lo: 2; x = x_hi * 2 + x_lo), y: 4, z: 8, core: 2. Of those that a mesh axis runs over, the one named last changes fastest.
Arguments:
- x_rows: bfloat16 [131072, 1024], P(('dp', 'expert')), may hold values from -24 to 24
- dy_rows: bfloat16 [131072, 2048], P(('dp', 'expert')), may hold values from -0.0234375 to 0.0234375
- seg_blocks: int32 [256, 8], replicated, may hold values from 0 to 2, as said below
Outputs:
- expert_grad: float32 [8, 1024, 2048], P(None, 'dp', 'expert')
Inputs may be any that keep to these rules, and one draw needn't show every extreme that they name: `seg_blocks`: on every device the entries sum to at most 4; one expert has exactly 2 blocks on every device.
All inputs are finite; a program needn't handle non-finite values.
Results may differ from a plain program's by a relative error of at most 0.0003.
Values may be sent and summed in bfloat16 or wider, within the bound.
A program may use at most 128 MiB of HBM per device.

v0:
```python
import jax
import jax.numpy as jnp
from jax import lax
from jax.sharding import PartitionSpec as P

BLOCK = 128


def row_owners(seg_blocks, devices, nblk):
    counts = seg_blocks[devices]
    ends = jnp.cumsum(counts, axis=1)
    block = jnp.arange(nblk, dtype=jnp.int32)
    return jnp.sum((ends[:, None, :] <= block[None, :, None]).astype(jnp.int32), axis=2)


def shards(x_rows, dy_rows, seg_blocks):
    rows, hid = x_rows.shape
    ffn = dy_rows.shape[1]
    n_exp = lax.axis_size("expert")
    experts = seg_blocks.shape[1]
    nblk = rows // BLOCK
    devices = lax.axis_index("dp") * n_exp + jnp.arange(n_exp)
    owner = row_owners(seg_blocks, devices, nblk).reshape(-1)
    mask = (owner[None, :] == jnp.arange(experts)[:, None]).astype(x_rows.dtype)
    mask = jnp.repeat(mask, BLOCK, axis=1)
    xg = lax.all_gather(x_rows, "expert", axis=0, tiled=True)
    dyg = lax.all_to_all(dy_rows, "expert", split_axis=1, concat_axis=0, tiled=True)
    xm = xg[None] * mask[:, :, None]
    part = jnp.einsum("eth,tf->ehf", xm, dyg, preferred_element_type=jnp.float32)
    return lax.psum_scatter(part, "dp", scatter_dimension=1, tiled=True)


def solution(mesh):
    in_specs = (P(("dp", "expert"), None), P(("dp", "expert"), None), P())
    out_specs = P(None, "dp", "expert")
    return jax.shard_map(shards, mesh=mesh, in_specs=in_specs, out_specs=out_specs, check_vma=False)
```

profile of v0, /device:TPU:8, one launch (start us, length us, event | category | flops | bytes accessed | tf_op | source)
XLA Modules:
  0.0 318.6 jit_solution(7816214932795877325)
XLA Ops:
  6.5 0.0 copy-start
  6.5 0.0 all-gather.2.cloned.1.call-start
  6.5 0.7 all-gather.2.cloned.1.call-update
  7.3 3.1 copy.16
  10.3 5.8 %all-to-all-start = ((bf16[512,8,256]{2,0,1:T(8,128)(2,1)}), bf16[512,8,256]{2,0,1:T(8,128)(2,1)S(1)}, u32[]{:S(2)}, u32[]{:S(2)}) async-start(bf16[512,8,256]{2,0,1:T(8,128)(2,1)} %bitcast.13), calls=%async_computation | async-start | bytes 4194304 | tf_op jit(solution)/shard_map/all_to_all | solution.py:27
  16.2 0.0 reduce-scatter.2.cloned.1.call-start
  16.2 0.0 copy-done
  16.2 0.1 copy.11
  16.3 0.6 gather_fusion
  16.9 0.2 reduce_window_sum.11
  17.1 0.1 convert_reduce_fusion
  17.2 0.1 copy.12
  17.3 0.1 eq.15
  17.4 0.1 fusion.4
  17.4 0.1 broadcast_bitcast_fusion
  17.6 102.1 %all-gather.2.cloned.1.call-done = bf16[4096,1024]{1,0:T(8,128)(2,1)} async-done(((bf16[512,1024]{1,0:T(8,128)(2,1)}), bf16[4096,1024]{1,0:T(8,128)(2,1)}) %all-gather.2.cloned.1.call-update) | async-done | bytes 8388624 | tf_op jit(solution)/shard_map/all_gather | solution.py:26
  119.6 11.8 %copy.10 = bf16[4096,1024]{0,1:T(8,128)(2,1)} copy(bf16[4096,1024]{1,0:T(8,128)(2,1)} %all-gather.2.cloned.1.call-done) | data formatting | bytes 16777216 | tf_op jit(solution)/shard_map/all_gather | solution.py:26
  131.4 0.0 all-to-all-done
  131.4 22.7 %fusion = f32[8,1024,256]{2,1,0:T(8,128)} fusion(bf16[4096,256,1]{1,0,2:T(8,128)(2,1)S(1)} %bitcast.15, bf16[8,4096]{1,0:T(8,128)(2,1)S(1)} %broadcast_bitcast_fusion, bf16[4096,1024]{0,1:T(8,128)(2,1)} %copy.10), kind=kOutput, calls=%fused_computation.1 | convolution fusion | flops 17213423616 | bytes 18939904 | tf_op jit(solution)/shard_map/eth,tf->ehf/dot_general | solution.py:29
  154.2 0.0 reduce-scatter.2.cloned.1.call-update
  154.2 157.6 %reduce-scatter.2.cloned.1.call-done = f32[8,32,256]{2,1,0:T(8,128)} async-done(((f32[8,1024,256]{2,1,0:T(8,128)}), f32[8,32,256]{2,1,0:T(8,128)}) %reduce-scatter.2.cloned.1.call-update) | async-done | bytes 262160 | tf_op jit(solution)/shard_map/reduce_scatter | solution.py:30
  (2 shorter events, 0.0 us)
Async XLA Ops:
  6.5 9.6 %copy-start = (s32[256,8]{0,1:T(8,128)S(1)}, s32[256,8]{0,1:T(8,128)}, u32[]{:S(2)}) copy-start(s32[256,8]{0,1:T(8,128)} %param.5) | copy-start | bytes 24580
  6.5 113.1 %all-gather.2.cloned.1.call-start = ((), (), s32[]{:S(2)}) async-start(), calls=%async_computation.2 | async-start | bytes 9437184 | tf_op jit(solution)/shard_map/all_gather | solution.py:26
  10.3 121.1 %all-to-all-start = ((bf16[512,8,256]{2,0,1:T(8,128)(2,1)}), bf16[512,8,256]{2,0,1:T(8,128)(2,1)S(1)}, u32[]{:S(2)}, u32[]{:S(2)}) async-start(bf16[512,8,256]{2,0,1:T(8,128)(2,1)} %bitcast.13), calls=%async_computation | async-start | bytes 4194304 | tf_op jit(solution)/shard_map/all_to_all | solution.py:27
  16.2 295.6 %reduce-scatter.2.cloned.1.call-start = ((), (), s32[]{:S(2)}) async-start(), calls=%async_computation.3 | async-start | bytes 8650752 | tf_op jit(solution)/shard_map/reduce_scatter | solution.py:30
Sparse Core Ops, SparseCore 0:
  9.1 110.4 all-gather.1
  154.3 157.4 reduce-scatter.1
where the time goes:
time: 319 us
  waiting for transfers between devices  260 us (82%)
  matrix products  22.7 us (7%)
  local copies, waits for them, and re-layouts  15.8 us (5%)
  between operations  13.4 us (4%)
  starting transfers between devices  5.85 us (2%)
    reduce_scatter x1, waiting for transfers between devices, shards(): return lax.psum_scatter(part, 'dp', scatter_dimension=1, tiled=True)  158 us
    all_gather x1, waiting for transfers between devices, shards(): xg = lax.all_gather(x_rows, 'expert', axis=0, tiled=True)  102 us
    dot_general x1, matrix products, shards(): jnp.einsum('eth,tf->ehf', xm, dyg, preferred_element_type=jnp.float32)  22.7 us
    all_gather x1, local copies, waits for them, and re-layouts, shards(): xg = lax.all_gather(x_rows, 'expert', axis=0, tiled=True)  11.8 us
  transfers between devices with their start and end apart: 3, of which 2 were waited for; matrix products, arithmetic and copies ran while one was open for 5% of the time, Pallas kernels for 0%

commit v1 on v0

--- a/solution.py
+++ b/solution.py
@@ -23,7 +23,9 @@
     owner = row_owners(seg_blocks, devices, nblk).reshape(-1)
     mask = (owner[None, :] == jnp.arange(experts)[:, None]).astype(x_rows.dtype)
     mask = jnp.repeat(mask, BLOCK, axis=1)
-    xg = lax.all_gather(x_rows, "expert", axis=0, tiled=True)
+    xg = jnp.concatenate(
+        lax.all_to_all(jnp.stack([x_rows] * lax.axis_size("expert")), "expert", 0, 0), axis=0
+    )
     dyg = lax.all_to_all(dy_rows, "expert", split_axis=1, concat_axis=0, tiled=True)
     xm = xg[None] * mask[:, :, None]
     part = jnp.einsum("eth,tf->ehf", xm, dyg, preferred_element_type=jnp.float32)

time: 319 us -> 327 us (1.025)
  local copies, waits for them, and re-layouts: 15.8 us -> 31.1 us
  waiting for transfers between devices: 260 us -> 247 us
  starting transfers between devices: 5.85 us -> 11.9 us
    all_gather x1 -> x0, waiting for transfers between devices: 102 us -> none  [shards(): xg = lax.all_gather(x_rows, 'expert', axis=0, tiled=True)]
    all_to_all x0 -> x1, waiting for transfers between devices: none -> 89.8 us  [shards(): lax.all_to_all(jnp.stack([x_rows] * lax.axis_size('expert')), 'expert', 0...]
    all_gather x1 -> x0, local copies, waits for them, and re-layouts: 11.8 us -> none  [shards(): xg = lax.all_gather(x_rows, 'expert', axis=0, tiled=True)]
    mul x1 -> x2, local copies, waits for them, and re-layouts: 0.11 us -> 11.9 us  [shards(): xm = xg[None] * mask[:, :, None]]
    all_to_all x0 -> x1, local copies, waits for them, and re-layouts: none -> 11.4 us  [shards(): lax.all_to_all(jnp.stack([x_rows] * lax.axis_size('expert')), 'expert', 0...]
    all_to_all x0 -> x1, starting transfers between devices: none -> 7.12 us  [shards(): lax.all_to_all(jnp.stack([x_rows] * lax.axis_size('expert')), 'expert', 0...]
    another operation x0 -> x1, local copies, waits for them, and re-layouts: none -> 3.93 us  [shards(): jnp.stack([x_rows] * lax.axis_size('expert'))]
  transfers between devices with their start and end apart: 3 -> 3, of which waited for: 2 -> 3; matrix products, arithmetic and copies ran while one was open for 5% -> 8% of each run, Pallas kernels for 0% -> 0%
where the time goes in v1:
time: 327 us
  waiting for transfers between devices  247 us (76%)
  local copies, waits for them, and re-layouts  31.1 us (10%)
  matrix products  22.7 us (7%)
  between operations  13.4 us (4%)
  starting transfers between devices  11.9 us (4%)
    reduce_scatter x1, waiting for transfers between devices, shards(): return lax.psum_scatter(part, 'dp', scatter_dimension=1, tiled=True)  157 us
    all_to_all x1, waiting for transfers between devices, shards(): lax.all_to_all(jnp.stack([x_rows] * lax.axis_size('expert')), 'expert', 0...  89.8 us
    dot_general x1, matrix products, shards(): jnp.einsum('eth,tf->ehf', xm, dyg, preferred_element_type=jnp.float32)  22.7 us
    mul x2, local copies, waits for them, and re-layouts, shards(): xm = xg[None] * mask[:, :, None]  11.9 us
    all_to_all x1, local copies, waits for them, and re-layouts, shards(): lax.all_to_all(jnp.stack([x_rows] * lax.axis_size('expert')), 'expert', 0...  11.4 us
    all_to_all x1, starting transfers between devices, shards(): lax.all_to_all(jnp.stack([x_rows] * lax.axis_size('expert')), 'expert', 0...  7.12 us
  transfers between devices with their start and end apart: 3, of which 3 were waited for; matrix products, arithmetic and copies ran while one was open for 8% of the time, Pallas kernels for 0%

profile of v1, /device:TPU:8, one launch (start us, length us, event | category | flops | bytes accessed | tf_op | source)
XLA Modules:
  0.0 326.6 jit_solution(7291848962680760954)
XLA Ops:
  6.5 1.5 copy.18
  8.0 3.9 %stack.2 = bf16[8,512,1024]{1,2,0:T(8,128)(2,1)} broadcast(bf16[512,1024]{0,1:T(8,128)(2,1)S(1)} %copy.18), dimensions={1,2} | broadcast | bytes 9437184 | tf_op jit(solution)/shard_map/stack | solution.py:27
  12.0 0.0 copy-start
  12.0 7.1 %all-to-all-start = ((bf16[8,512,1024]{1,2,0:T(8,128)(2,1)}), bf16[8,512,1024]{1,2,0:T(8,128)(2,1)}, u32[]{:S(2)}, u32[]{:S(2)}) async-start(bf16[8,512,1024]{1,2,0:T(8,128)(2,1)} %stack.2), calls=%async_computation | async-start | bytes 16777216 | tf_op jit(solution)/shard_map/all_to_all | solution.py:27
  19.1 0.0 copy-start.1
  19.1 0.0 copy-done
  19.1 1.5 copy.26
  20.6 89.8 %all-to-all-done = bf16[8,512,1024]{1,2,0:T(8,128)(2,1)} async-done(((bf16[8,512,1024]{1,2,0:T(8,128)(2,1)}), bf16[8,512,1024]{1,2,0:T(8,128)(2,1)}, u32[]{:S(2)}, u32[]{:S(2)}) %all-to-all-start) | async-done | bytes 8388640 | tf_op jit(solution)/shard_map/all_to_all | solution.py:27
  110.3 4.8 %all-to-all-start.1 = ((bf16[512,8,256]{2,0,1:T(8,128)(2,1)}), bf16[512,8,256]{2,0,1:T(8,128)(2,1)S(1)}, u32[]{:S(2)}, u32[]{:S(2)}) async-start(bf16[512,8,256]{2,0,1:T(8,128)(2,1)} %bitcast.14), calls=%async_computation.1 | async-start | bytes 4194304 | tf_op jit(solution)/shard_map/all_to_all | solution.py:29
  115.1 0.0 reduce-scatter.2.cloned.1.call-start
  115.1 0.0 copy-done.1
  115.1 0.1 copy.21
  115.3 0.6 gather_fusion
  115.9 0.2 reduce_window_sum.11
  116.0 0.1 convert_reduce_fusion
  116.2 0.1 copy.22
  116.2 0.1 eq.15
  116.3 0.1 fusion.4
  116.4 0.1 broadcast_bitcast_fusion
  116.5 11.4 %copy.19 = bf16[8,512,1024]{2,1,0:T(8,128)(2,1)} copy(bf16[8,512,1024]{1,2,0:T(8,128)(2,1)} %all-to-all-done) | data formatting | bytes 16777216 | tf_op jit(solution)/shard_map/all_to_all | solution.py:27
  128.0 11.8 %copy.20 = bf16[4096,1024]{0,1:T(8,128)(2,1)} copy(bf16[4096,1024]{1,0:T(8,128)(2,1)} %bitcast.15) | data formatting | bytes 16777216 | tf_op jit(solution)/shard_map/mul | solution.py:30
  139.8 0.4 all-to-all-done.1
  140.2 22.7 %fusion = f32[8,1024,256]{2,1,0:T(8,128)} fusion(bf16[4096,256,1]{1,0,2:T(8,128)(2,1)S(1)} %bitcast.17, bf16[8,4096]{1,0:T(8,128)(2,1)S(1)} %broadcast_bitcast_fusion, bf16[4096,1024]{0,1:T(8,128)(2,1)} %copy.20), kind=kOutput, calls=%fused_computation.1 | convolution fusion | flops 17213423616 | bytes 18939904 | tf_op jit(solution)/shard_map/eth,tf->ehf/dot_general | solution.py:31
  162.9 0.0 reduce-scatter.2.cloned.1.call-update
  162.9 156.8 %reduce-scatter.2.cloned.1.call-done = f32[8,32,256]{2,1,0:T(8,128)} async-done(((f32[8,1024,256]{2,1,0:T(8,128)}), f32[8,32,256]{2,1,0:T(8,128)}) %reduce-scatter.2.cloned.1.call-update) | async-done | bytes 262160 | tf_op jit(solution)/shard_map/reduce_scatter | solution.py:32
  (2 shorter events, 0.0 us)
Async XLA Ops:
  12.0 7.1 %copy-start = (bf16[512,2048]{1,0:T(8,128)(2,1)S(1)}, bf16[512,2048]{1,0:T(8,128)(2,1)}, u32[]{:S(2)}) copy-start(bf16[512,2048]{1,0:T(8,128)(2,1)} %param.4) | copy-start | bytes 6291460
  12.0 98.4 %all-to-all-start = ((bf16[8,512,1024]{1,2,0:T(8,128)(2,1)}), bf16[8,512,1024]{1,2,0:T(8,128)(2,1)}, u32[]{:S(2)}, u32[]{:S(2)}) async-start(bf16[8,512,1024]{1,2,0:T(8,128)(2,1)} %stack.2), calls=%async_computation | async-start | bytes 16777216 | tf_op jit(solution)/shard_map/all_to_all | solution.py:27
  19.1 96.0 %copy-start.1 = (s32[256,8]{0,1:T(8,128)S(1)}, s32[256,8]{0,1:T(8,128)}, u32[]{:S(2)}) copy-start(s32[256,8]{0,1:T(8,128)} %param.5) | copy-start | bytes 24580
  110.3 29.9 %all-to-all-start.1 = ((bf16[512,8,256]{2,0,1:T(8,128)(2,1)}), bf16[512,8,256]{2,0,1:T(8,128)(2,1)S(1)}, u32[]{:S(2)}, u32[]{:S(2)}) async-start(bf16[512,8,256]{2,0,1:T(8,128)(2,1)} %bitcast.14), calls=%async_computation.1 | async-start | bytes 4194304 | tf_op jit(solution)/shard_map/all_to_all | solution.py:29
  115.1 204.6 %reduce-scatter.2.cloned.1.call-start = ((), (), s32[]{:S(2)}) async-start(), calls=%async_computation.3 | async-start | bytes 8650752 | tf_op jit(solution)/shard_map/reduce_scatter | solution.py:32
Sparse Core Ops, SparseCore 0:
  163.1 156.6 reduce-scatter.1
